TPU v7x, 32 devices: a whole 2x2x4 slice. The times are simulated.
32 devices in a mesh: tau: 4 (over z), row: 4 (over y, core), col: 2 (over x).
Axes of the slice: x: 2, y: 2, z: 4, core: 2. Of those that a mesh axis runs over, the one named last changes fastest.
Arguments:
- occupied: bfloat16 [4, 1024, 8192], P('tau', 'row', 'col'), may hold values from -6 to 6
- virtual_green: bfloat16 [4, 8192, 2048], P('tau', 'row', 'col'), may hold values from -0.0625 to 0.0625
- occ_mask: int32 [8, 64], P('row', 'col'), may hold values 0 or 1
- virt_mask: int32 [64, 16], P('row', 'col'), may hold values 0 or 1
- chi_mask: int32 [8, 16], P('row', 'col'), may hold values 0 or 1
- cosine_weights: float32 [4, 4], replicated, may hold values from -3 to 3
Outputs:
- chi_freq: float32 [4, 1024, 2048], P(None, ('row', 'tau'), 'col')
All inputs are finite; a program needn't handle non-finite values. No bound on the sum of `occ_mask` or of `virt_mask` or of `chi_mask` on one device may be relied on, other than what follows from the above.
Results may differ from a plain program's by a relative error of at most 0.0029.
Values may be sent and summed in bfloat16 or wider, within the bound.
A program may use at most 64 MiB of HBM per device.

v0:
```python
import jax
import jax.numpy as jnp
from jax import lax
from jax.sharding import PartitionSpec as P


def expand_mask(values, flags):
    block_rows = values.shape[0] // flags.shape[0]
    block_cols = values.shape[1] // flags.shape[1]
    shaped = values.reshape(flags.shape[0], block_rows, flags.shape[1], block_cols)
    masked = shaped * flags.astype(values.dtype)[:, None, :, None]
    return masked.reshape(values.shape)


def shards(occupied, virtual_green, occ_mask, virt_mask, chi_mask, cosine_weights):
    occ_tile = expand_mask(occupied[0], occ_mask)
    virt_tile = expand_mask(virtual_green[0], virt_mask)
    virt_column = lax.all_gather(virt_tile, "row", axis=0, tiled=True)
    accumulated = jnp.dot(
        lax.all_gather(occ_tile, "col", axis=1, tiled=True),
        virt_column,
        preferred_element_type=jnp.float32,
    )
    chi_local = expand_mask(accumulated, chi_mask).astype(jnp.bfloat16)
    regrouped = lax.all_to_all(chi_local[None], "tau", split_axis=1, concat_axis=0, tiled=True)
    return jnp.einsum(
        "kt,tij->kij",
        cosine_weights,
        regrouped.astype(jnp.float32),
        precision=lax.Precision.HIGHEST,
    )


def solution(mesh):
    placed = (
        P("tau", "row", "col"),
        P("tau", "row", "col"),
        P("row", "col"),
        P("row", "col"),
        P("row", "col"),
        P(),
    )
    return jax.shard_map(
        shards,
        mesh=mesh,
        in_specs=placed,
        out_specs=P(None, ("row", "tau"), "col"),
        check_vma=False,
    )
```

profile of v0, /device:TPU:0, one launch (start us, length us, event | category | flops | bytes accessed | tf_op | source)
XLA Modules:
  0.0 225.5 jit_solution(6269952776549928674)
XLA Ops:
  6.5 0.0 copy-start
  6.5 0.0 all-gather.3.cloned.1.call-start
  6.5 0.7 convert_element_type.13
  7.2 0.3 mul.33
  7.6 0.0 copy-start.2
  7.6 3.8 %bitcast_multiply_fusion.1 = bf16[256,4096]{1,0:T(8,128)(2,1)} fusion(bf16[32,8,32,128]{3,2,1,0:T(8,128)(2,1)S(1)} %bitcast.31, bf16[1,256,4096]{2,1,0:T(8,128)(2,1)} %param.6), kind=kLoop, calls=%fused_computation.1 | loop fusion | flops 1048576 | bytes 6291456 | tf_op jit(solution)/shard_map/mul | solution.py:11
  11.4 0.0 all-gather.3.cloned.1.call-update
  11.4 0.0 all-gather.5.cloned.1.call-start
  11.5 0.0 copy-done.2
  11.5 0.1 copy.13
  11.6 0.0 copy-start.1
  11.6 0.6 mul.36
  12.2 1.6 copy-done.1
  13.8 2.5 %bitcast_multiply_fusion = bf16[2048,1024]{1,0:T(8,128)(2,1)} fusion(bf16[256,8,8,128]{3,2,1,0:T(8,128)(2,1)S(1)} %bitcast.30, bf16[1,2048,1024]{2,1,0:T(8,128)(2,1)S(1)} %copy-done.1), kind=kLoop, calls=%fused_computation | loop fusion | flops 2097152 | bytes 12582912 | tf_op jit(solution)/shard_map/mul | solution.py:11
  16.3 0.0 copy-start.3
  16.3 0.0 all-gather.5.cloned.1.call-update
  16.3 0.7 copy-done.3
  17.0 54.0 %all-gather.3.cloned.1.call-done = bf16[256,8192]{1,0:T(8,128)(2,1)} async-done(((bf16[256,4096]{1,0:T(8,128)(2,1)}), bf16[256,8192]{1,0:T(8,128)(2,1)}) %all-gather.3.cloned.1.call-update) | async-done | bytes 4194320 | tf_op jit(solution)/shard_map/all_gather | solution.py:20
  71.0 107.5 %all-gather.5.cloned.1.call-done = bf16[8192,1024]{1,0:T(8,128)(2,1)} async-done(((bf16[2048,1024]{1,0:T(8,128)(2,1)}), bf16[8192,1024]{1,0:T(8,128)(2,1)}) %all-gather.5.cloned.1.call-update) | async-done | bytes 16777232 | tf_op jit(solution)/shard_map/all_gather | solution.py:18
  178.5 0.1 mul.39
  178.7 11.6 %fusion.1 = bf16[1,256,1024]{2,1,0:T(8,128)(2,1)S(1)} fusion(bf16[256,8192]{1,0:T(8,128)(2,1)} %all-gather.3.cloned.1.call-done, bf16[8192,1024]{1,0:T(8,128)(2,1)} %all-gather.5.cloned.1.call-done, f32[32,8,8,128]{3,2,1,0:T(8,128)S(1)} %bitcast.35), kind=kOutput, calls=%fused_computation.5 | convolution fusion | flops 4295491584 | bytes 22544384 | tf_op jit(solution)/shard_map/dot_general | solution.py:19
  190.3 0.8 copy.27
  191.1 0.5 broadcast.6
  191.6 3.9 %reduce = bf16[256,1024]{1,0:T(8,128)(2,1)S(1)} reduce(bf16[256,1,1024]{2,1,0:T(2,128)(2,1)S(1)} %bitcast.33, bf16[]{:T(256)} %broadcast.6), dimensions={1}, to_apply=%bitcast.29.reduce_sub_computation | reduce | bytes 1048578
  195.5 0.4 reshape.16
  195.9 19.3 %all_to_all.12 = bf16[4,2,32768]{2,1,0:T(2,128)(2,1)S(1)} all-to-all(bf16[4,2,32768]{2,1,0:T(2,128)(2,1)S(1)} %reshape.16), channel_id=1, replica_groups=mesh['tau'=4,'row'=4,'col'=2] {'tau'}, dimensions={0} | all-to-all | bytes 1048576 | tf_op jit(solution)/shard_map/all_to_all | solution.py:25
  215.2 0.5 reshape.17
  215.8 0.2 copy.17
  215.9 0.0 copy-done
  215.9 1.1 convolution_bitcast_fusion
  217.1 1.6 copy.16
  (2 shorter events, 0.0 us)
Async XLA Ops:
  6.5 209.4 %copy-start = (f32[4,4]{1,0:T(4,128)S(1)}, f32[4,4]{1,0:T(4,128)}, u32[]{:S(2)}) copy-start(f32[4,4]{1,0:T(4,128)} %param.11) | copy-start | bytes 196
  6.5 64.5 %all-gather.3.cloned.1.call-start = ((), (), s32[]{:S(2)}) async-start(), calls=%async_computation.1 | async-start | bytes 6291456 | tf_op jit(solution)/shard_map/all_gather | solution.py:20
  7.6 3.9 %copy-start.2 = (s32[16,8]{0,1:T(8,128)S(1)}, s32[16,8]{0,1:T(8,128)}, u32[]{:S(2)}) copy-start(s32[16,8]{0,1:T(8,128)} %param.9) | copy-start | bytes 1540
  11.4 167.1 %all-gather.5.cloned.1.call-start = ((), (), s32[]{:S(2)}) async-start(), calls=%async_computation.2 | async-start | bytes 20971520 | tf_op jit(solution)/shard_map/all_gather | solution.py:18
  11.6 2.2 copy-start.1
  16.3 0.7 copy-start.3
Sparse Core Ops, SparseCore 0:
  11.6 59.4 all-gather.2
  72.6 105.8 all-gather.4
where the time goes:
time: 226 us; the launch traced here: 225 us
  waiting for transfers between devices  162 us (72%)
  blocking collectives  19.3 us (9%)
  between operations  13.5 us (6%)
  matrix products  12.7 us (6%)
  other arithmetic  11 us (5%)
  local copies, waits for them, and re-layouts  7.38 us (3%)
    all_gather x1, waiting for transfers between devices, shards(): virt_column = lax.all_gather(virt_tile, 'row', axis=0, tiled=True)  107 us
    all_gather x1, waiting for transfers between devices, shards(): lax.all_gather(occ_tile, 'col', axis=1, tiled=True)  54 us
    all_to_all x1, blocking collectives, shards(): lax.all_to_all(chi_local[None], 'tau', split_axis=1, concat_axis=0, tiled...  19.3 us
    dot_general x1, matrix products, shards(): jnp.dot(lax.all_gather(occ_tile, 'col', axis=1, tiled=True), virt_column,...  11.6 us
    mul x2, other arithmetic, expand_mask(): masked = shaped * flags.astype(values.dtype)[:, None, :, None]  6.35 us
  transfers between devices with their start and end apart: 2, of which 2 were waited for; matrix products, arithmetic and copies ran while one was open for 1% of the time, Pallas kernels for 0%

commit v1 on v0

--- a/solution.py
+++ b/solution.py
@@ -1,7 +1,13 @@
+import functools
+
 import jax
 import jax.numpy as jnp
 from jax import lax
+from jax.experimental import pallas as pl
+from jax.experimental.pallas import tpu as pltpu
 from jax.sharding import PartitionSpec as P
+
+MESH = pl.DeviceIdType.MESH
 
 
 def expand_mask(values, flags):
@@ -12,7 +18,7 @@
     return masked.reshape(values.shape)
 
 
-def shards(occupied, virtual_green, occ_mask, virt_mask, chi_mask, cosine_weights):
+def gathered(occupied, virtual_green, occ_mask, virt_mask, chi_mask, cosine_weights):
     occ_tile = expand_mask(occupied[0], occ_mask)
     virt_tile = expand_mask(virtual_green[0], virt_mask)
     virt_column = lax.all_gather(virt_tile, "row", axis=0, tiled=True)
@@ -29,6 +35,223 @@
         regrouped.astype(jnp.float32),
         precision=lax.Precision.HIGHEST,
     )
+
+
+def kernel(
+    taus, occ, virt, om, vm, cm, w, out,
+    vbuf, vmask, ob, omask, lhs, pa, pbuf, rbuf, cbuf, zbuf,
+    v_sem, o_send, o_recv, m_send, m_recv, p_send, p_recv, z_send, z_recv,
+):
+    tau, row, col = lax.axis_index("tau"), lax.axis_index("row"), lax.axis_index("col")
+    half, core = row // 2, row % 2
+    diagonal = half == col
+    flipped = (1 - half) * 2 + core
+    x_peer = {"tau": tau, "row": row, "col": 1 - col}
+    y_peer = {"tau": tau, "row": flipped, "col": col}
+    far_peer = {"tau": tau, "row": flipped, "col": 1 - col}
+    twin = {"tau": tau, "row": half * 2 + 1 - core, "col": col}
+    rows = ob.shape[2]
+    depth = virt.shape[0]
+    block = occ.shape[0] // om.shape[0]
+    cols = virt.shape[1]
+
+    def part(step):
+        return lax.rem(tau + 1 + step, taus)
+
+    def z_peer(step):
+        return {"tau": part(step), "row": row, "col": col}
+
+    def remote(src, dst, send, recv, peer):
+        return pltpu.make_async_remote_copy(
+            src_ref=src, dst_ref=dst, send_sem=send, recv_sem=recv, device_id=peer, device_id_type=MESH
+        )
+
+    mine = pl.ds(pl.multiple_of(core * depth, depth), depth)
+    v_local = pltpu.make_async_copy(virt, vbuf.at[mine, :], v_sem.at[0])
+    v_local.start()
+    vm_rows = vm.shape[0]
+    vm_mine = pl.ds(pl.multiple_of(core * vm_rows, vm_rows), vm_rows)
+    vm_local = pltpu.make_async_copy(vm, vmask.at[vm_mine, :], v_sem.at[1])
+    vm_local.start()
+
+    barrier = pltpu.get_barrier_semaphore()
+    peers = [x_peer, y_peer, far_peer, twin] + [z_peer(s) for s in range(taus - 1)]
+    for peer in peers:
+        pl.semaphore_signal(barrier, inc=1, device_id=peer, device_id_type=MESH)
+    pl.semaphore_wait(barrier, len(peers))
+
+    def o_src(step):
+        return occ.at[pl.ds(pl.multiple_of(part(step) * rows, rows), rows), :]
+
+    def to_self(src, dst, sem):
+        return pltpu.make_async_copy(src, dst, sem)
+
+    def send_part(step):
+        src = o_src(step)
+
+        @pl.when(diagonal)
+        def _():
+            remote(src, ob.at[step, 1], o_send.at[step, 0], o_recv.at[step, 1], x_peer).start()
+            to_self(src, ob.at[step, 1], o_recv.at[step, 1]).start()
+
+        @pl.when(jnp.logical_not(diagonal))
+        def _():
+            remote(src, ob.at[step, 0], o_send.at[step, 1], o_recv.at[step, 0], far_peer).start()
+            remote(src, ob.at[step, 0], o_send.at[step, 0], o_recv.at[step, 0], y_peer).start()
+
+    @pl.when(diagonal)
+    def _():
+        remote(om, omask.at[1], m_send.at[0], m_recv.at[1], x_peer).start()
+        to_self(om, omask.at[1], m_recv.at[1]).start()
+
+    @pl.when(jnp.logical_not(diagonal))
+    def _():
+        remote(om, omask.at[0], m_send.at[1], m_recv.at[0], far_peer).start()
+        remote(om, omask.at[0], m_send.at[0], m_recv.at[0], y_peer).start()
+
+    send_part(0)
+    v_remote = remote(virt, vbuf.at[mine, :], v_sem.at[2], v_sem.at[3], twin)
+    v_remote.start()
+    vm_remote = remote(vm, vmask.at[vm_mine, :], v_sem.at[4], v_sem.at[5], twin)
+    vm_remote.start()
+    if taus > 1:
+        send_part(1)
+
+    deep = depth // vm_rows
+
+    def mask_virt(base):
+        def one(b, _):
+            r = pl.ds(pl.multiple_of((base + b) * deep, deep), deep)
+            flags = vmask[pl.ds(base + b, 1), :]
+            vbuf[r, :] = vbuf[r, :] * jnp.broadcast_to(flags, (deep, cols)).astype(vbuf.dtype)
+            return 0
+
+        lax.fori_loop(0, vm_rows, one, 0)
+
+    v_local.wait()
+    vm_local.wait()
+    mask_virt(core * vm_rows)
+    v_remote.wait_recv()
+    vm_remote.wait_recv()
+    mask_virt((1 - core) * vm_rows)
+    for slot in range(2):
+        to_self(om, omask.at[slot], m_recv.at[slot]).wait()
+
+    tile = 256
+
+    def partial_copy(step):
+        return remote(pbuf.at[step], rbuf.at[step], p_send.at[step], p_recv.at[step], y_peer)
+
+    def z_copy(step):
+        return remote(cbuf.at[step], zbuf.at[tau], z_send.at[step], z_recv.at[step], z_peer(step))
+
+    def flag_row(step):
+        return part(step) * rows // block
+
+    def finish(step):
+        partial_copy(step).wait_recv()
+        flags = jnp.broadcast_to(cm[pl.ds(flag_row(step), 1), :], (rows, cols))
+        chi = ((pa[step] + rbuf[step].astype(jnp.float32)) * flags).astype(jnp.bfloat16)
+        if step < taus - 1:
+            cbuf[step] = chi
+            z_copy(step).start()
+        else:
+            zbuf[tau] = chi
+
+    for step in range(taus):
+        for slot in range(2):
+            to_self(o_src(step), ob.at[step, slot], o_recv.at[step, slot]).wait()
+            flags = omask[slot, pl.ds(flag_row(step), 1), :]
+            lhs[pl.ds(slot * rows, rows), :] = ob[step, slot] * jnp.broadcast_to(
+                flags, (rows, lhs.shape[1])
+            ).astype(lhs.dtype)
+
+        def one(n, _, step=step):
+            c = pl.ds(pl.multiple_of(n * tile, tile), tile)
+            r = jnp.dot(lhs[...], vbuf[:, c], preferred_element_type=jnp.float32)
+            pbuf[step, :, c] = r[:rows].astype(jnp.bfloat16)
+            pa[step, :, c] = r[rows:]
+            return 0
+
+        lax.fori_loop(0, cols // tile, one, 0)
+        partial_copy(step).start()
+        if step + 2 < taus:
+            send_part(step + 2)
+        if step > 0:
+            finish(step - 1)
+    finish(taus - 1)
+
+    for step in range(taus - 1):
+        z_copy(step).wait_recv()
+    for k in range(out.shape[0]):
+        total = w[k, 0] * zbuf[0].astype(jnp.float32)
+        for t in range(1, taus):
+            total = total + w[k, t] * zbuf[t].astype(jnp.float32)
+        out[k] = total
+
+    for step in range(taus - 1):
+        z_copy(step).wait_send()
+    for step in range(taus):
+        partial_copy(step).wait_send()
+        remote(o_src(step), ob.at[step, 1], o_send.at[step, 0], o_recv.at[step, 1], x_peer).wait_send()
+    remote(om, omask.at[1], m_send.at[0], m_recv.at[1], x_peer).wait_send()
+
+    @pl.when(jnp.logical_not(diagonal))
+    def _():
+        for step in range(taus):
+            remote(o_src(step), ob.at[step, 0], o_send.at[step, 1], o_recv.at[step, 0], far_peer).wait_send()
+        remote(om, omask.at[0], m_send.at[1], m_recv.at[0], far_peer).wait_send()
+
+    v_remote.wait_send()
+    vm_remote.wait_send()
+
+
+def exchanged(taus, occupied, virtual_green, occ_mask, virt_mask, chi_mask, cosine_weights):
+    occ, virt = occupied[0], virtual_green[0]
+    m, k = occ.shape
+    depth, cols = virt.shape
+    rows = m // taus
+    om = jnp.repeat(occ_mask.astype(jnp.float32), k // occ_mask.shape[1], axis=1)
+    vm = jnp.repeat(virt_mask.astype(jnp.float32), cols // virt_mask.shape[1], axis=1)
+    cm = jnp.repeat(chi_mask.astype(jnp.float32), cols // chi_mask.shape[1], axis=1)
+    bf16, f32 = jnp.bfloat16, jnp.float32
+    dma = pltpu.SemaphoreType.DMA
+    vmem = pl.BlockSpec(memory_space=pltpu.VMEM)
+    return pl.pallas_call(
+        functools.partial(kernel, taus),
+        out_shape=jax.ShapeDtypeStruct((cosine_weights.shape[0], rows, cols), f32),
+        in_specs=[
+            pl.BlockSpec(memory_space=pl.ANY),
+            pl.BlockSpec(memory_space=pl.ANY),
+            vmem,
+            vmem,
+            vmem,
+            pl.BlockSpec(memory_space=pltpu.SMEM),
+        ],
+        out_specs=vmem,
+        scratch_shapes=[
+            pltpu.VMEM((2 * depth, cols), bf16),
+            pltpu.VMEM((2 * vm.shape[0], cols), f32),
+            pltpu.VMEM((taus, 2, rows, k), bf16),
+            pltpu.VMEM((2,) + om.shape, f32),
+            pltpu.VMEM((2 * rows, k), bf16),
+            pltpu.VMEM((taus, rows, cols), f32),
+            pltpu.VMEM((taus, rows, cols), bf16),
+            pltpu.VMEM((taus, rows, cols), bf16),
+            pltpu.VMEM((taus, rows, cols), bf16),
+            pltpu.VMEM((taus, rows, cols), bf16),
+            dma((6,)),
+            dma((taus, 2)),
+            dma((taus, 2)),
+            dma((2,)),
+            dma((2,)),
+            dma((taus,)),
+            dma((taus,)),
+            dma((taus,)),
+            dma((taus,)),
+        ],
+        compiler_params=pltpu.CompilerParams(collective_id=0, has_side_effects=True),
+    )(occ, virt, om, vm, cm, cosine_weights)
 
 
 def solution(mesh):
@@ -40,8 +263,9 @@
         P("row", "col"),
         P(),
     )
+    plane = mesh.shape["row"] == 4 and mesh.shape["col"] == 2
     return jax.shard_map(
-        shards,
+        functools.partial(exchanged, mesh.shape["tau"]) if plane else gathered,
         mesh=mesh,
         in_specs=placed,
         out_specs=P(None, ("row", "tau"), "col"),

time: 226 us -> 76.3 us (0.34)
  waiting for transfers between devices: 162 us -> 0 us
  Pallas kernels: 0 us -> 69.1 us
  blocking collectives: 19.3 us -> 0 us
  between operations: 13.5 us -> 0.01 us
  matrix products: 12.7 us -> 0 us
  other arithmetic: 11 us -> 2.05 us
  local copies, waits for them, and re-layouts: 7.38 us -> 4.48 us
    all_gather x2 -> x0, waiting for transfers between devices: 162 us -> none  [the longest x1 107 us: shards(): virt_column = lax.all_gather(virt_tile, 'row', axis=0, tiled=True)]
    pallas_call x0 -> x1, Pallas kernels: none -> 69.1 us  [exchanged(): pl.pallas_call(functools.partial(kernel, taus), out_shape=jax.ShapeDtypeS...]
    all_to_all x1 -> x0, blocking collectives: 19.3 us -> none  [shards(): lax.all_to_all(chi_local[None], 'tau', split_axis=1, concat_axis=0, tiled...]
    dot_general x2 -> x0, matrix products: 12.7 us -> none  [the longest x1 11.6 us: shards(): jnp.dot(lax.all_gather(occ_tile, 'col', axis=1, tiled=True), virt_column,...]
    mul x2 -> x0, other arithmetic: 6.35 us -> none  [expand_mask(): masked = shaped * flags.astype(values.dtype)[:, None, :, None]]
    unnamed x1 -> x0, other arithmetic: 3.95 us -> none
  transfers between devices with their start and end apart: 2 -> 0, of which waited for: 2 -> 0; matrix products, arithmetic and copies ran while one was open for 1% -> 0% of each run, Pallas kernels for 0% -> 0%
where the time goes in v1:
time: 76.3 us; the launch traced here: 75.6 us
  Pallas kernels  69.1 us (91%)
  local copies, waits for them, and re-layouts  4.48 us (6%)
  other arithmetic  2.05 us (3%)
    pallas_call x1, Pallas kernels, exchanged(): pl.pallas_call(functools.partial(kernel, taus), out_shape=jax.ShapeDtypeS...  69.1 us
    unnamed x6, local copies, waits for them, and re-layouts  4.33 us

profile of v1, /device:TPU:0, one launch (start us, length us, event | category | flops | bytes accessed | tf_op | source)
XLA Modules:
  0.0 75.6 jit_solution(11816556011825845446)
XLA Ops:
  0.0 0.7 convert_element_type.9
  0.7 0.7 convert_element_type.11
  1.4 0.7 convert_element_type.10
  2.1 0.1 copy.7
  2.1 0.1 broadcast_bitcast_fusion.1
  2.2 0.6 copy.16
  2.8 0.1 broadcast_bitcast_fusion
  2.9 0.6 copy.15
  3.5 0.1 broadcast_in_dim.10
  3.6 0.7 copy.14
  4.2 69.1 %shard_map.64 = f32[4,64,1024]{2,1,0:T(8,128)} custom-call(bf16[256,4096]{1,0:T(8,128)(2,1)} %bitcast.17, bf16[2048,1024]{1,0:T(8,128)(2,1)} %bitcast.16, f32[2,4096]{1,0:T(2,128)} %bitcast.20, f32[16,1024]{1,0:T(8,128)} %bitcast.18, f32[2,1024]{1,0:T(2,128)} %bitcast.21, f32[4,4]{1,0:T(4,128)} %w.1), custom_call_target="tpu_custom_call" | custom-call | tf_op jit(solution)/shard_map/pallas_call | solution.py:220
  73.3 2.3 %copy.18 = f32[4,64,1024]{2,1,0:T(8,128)} copy(f32[4,64,1024]{2,1,0:T(8,128)} %shard_map.64) | data formatting | bytes 2097152

commit v2 on v0

--- a/solution.py
+++ b/solution.py
@@ -1,7 +1,13 @@
+import functools
+
 import jax
 import jax.numpy as jnp
 from jax import lax
+from jax.experimental import pallas as pl
+from jax.experimental.pallas import tpu as pltpu
 from jax.sharding import PartitionSpec as P
+
+MESH = pl.DeviceIdType.MESH
 
 
 def expand_mask(values, flags):
@@ -12,7 +18,7 @@
     return masked.reshape(values.shape)
 
 
-def shards(occupied, virtual_green, occ_mask, virt_mask, chi_mask, cosine_weights):
+def gathered(occupied, virtual_green, occ_mask, virt_mask, chi_mask, cosine_weights):
     occ_tile = expand_mask(occupied[0], occ_mask)
     virt_tile = expand_mask(virtual_green[0], virt_mask)
     virt_column = lax.all_gather(virt_tile, "row", axis=0, tiled=True)
@@ -29,6 +35,299 @@
         regrouped.astype(jnp.float32),
         precision=lax.Precision.HIGHEST,
     )
+
+
+def spread(flags, width, transposed=False):
+    dim = 0 if transposed else 1
+    count = flags.shape[dim]
+    owner = lax.broadcasted_iota(jnp.int32, (count, count * width), 1) // width
+    mine = owner == lax.broadcasted_iota(jnp.int32, (count, count * width), 0)
+    return lax.dot_general(
+        flags.astype(jnp.float32),
+        mine.astype(jnp.float32),
+        (((dim,), (0,)), ((), ())),
+        preferred_element_type=jnp.float32,
+    )
+
+
+def kernel(
+    taus, occ, virt, om, vm, cm, zbuf,
+    vbuf, vraw, vmask, ob, oraw, omask, cmask, lhs, pa, pbuf, rbuf, cbuf,
+    v_sem, o_send, o_recv, f_send, m_send, m_recv, p_send, p_recv, z_send, z_recv,
+):
+    tau, row, col = lax.axis_index("tau"), lax.axis_index("row"), lax.axis_index("col")
+    half, core = row // 2, row % 2
+    diagonal = half == col
+    flipped = (1 - half) * 2 + core
+    x_peer = {"tau": tau, "row": row, "col": 1 - col}
+    y_peer = {"tau": tau, "row": flipped, "col": col}
+    far_peer = {"tau": tau, "row": flipped, "col": 1 - col}
+    twin = {"tau": tau, "row": half * 2 + 1 - core, "col": col}
+    steps = 2 * taus
+    rows = ob.shape[2]
+    depth = virt.shape[0]
+    block = occ.shape[0] // om.shape[0]
+    cols = virt.shape[1]
+    near_only, far_only = 2, 3
+
+    def start_row(step):
+        return lax.rem(tau + 1 + step // 2, taus) * (2 * rows) + (step % 2) * rows
+
+    def z_peer(step):
+        return {"tau": lax.rem(tau + 1 + step // 2, taus), "row": row, "col": col}
+
+    def remote(src, dst, send, recv, peer):
+        return pltpu.make_async_remote_copy(
+            src_ref=src, dst_ref=dst, send_sem=send, recv_sem=recv, device_id=peer, device_id_type=MESH
+        )
+
+    mine = pl.ds(pl.multiple_of(core * depth, depth), depth)
+    v_local = pltpu.make_async_copy(virt, vbuf.at[mine, :], v_sem.at[0])
+    v_local.start()
+
+    barrier = pltpu.get_barrier_semaphore()
+    peers = [x_peer, y_peer, far_peer, twin] + [z_peer(2 * s) for s in range(taus - 1)]
+    for peer in peers:
+        pl.semaphore_signal(barrier, inc=1, device_id=peer, device_id_type=MESH)
+    pl.semaphore_wait(barrier, len(peers))
+
+    def o_src(step):
+        return occ.at[pl.ds(pl.multiple_of(start_row(step), rows), rows), :]
+
+    def on_diagonal(step):
+        return remote(o_src(step), ob.at[step, 1], o_send.at[step, 0], o_recv.at[step, 1], x_peer)
+
+    def own(step):
+        return pltpu.make_async_copy(o_src(step), ob.at[step, 1], o_recv.at[step, 1])
+
+    def near(step):
+        return remote(o_src(step), ob.at[step, 0], o_send.at[step, 0], o_recv.at[step, 0], y_peer)
+
+    def far(step):
+        return remote(o_src(step), ob.at[step, 0], o_send.at[step, 1], o_recv.at[step, 0], far_peer)
+
+    def forward(step):
+        return remote(ob.at[step, 0], ob.at[step, 0], f_send.at[0], o_recv.at[step, 0], x_peer)
+
+    def arrived(step, slot):
+        return pltpu.make_async_copy(o_src(step), ob.at[step, slot], o_recv.at[step, slot])
+
+    m_x = remote(om, oraw.at[1], m_send.at[0], m_recv.at[1], x_peer)
+    m_own = pltpu.make_async_copy(om, oraw.at[1], m_recv.at[1])
+    m_near = remote(om, oraw.at[0], m_send.at[0], m_recv.at[0], y_peer)
+    m_far = remote(om, oraw.at[0], m_send.at[1], m_recv.at[0], far_peer)
+    v_remote = remote(virt, vbuf.at[mine, :], v_sem.at[1], v_sem.at[2], twin)
+    vm_remote = remote(vm, vraw, v_sem.at[3], v_sem.at[4], twin)
+
+    @pl.when(diagonal)
+    def _():
+        m_x.start()
+        m_own.start()
+        for step in (0, 1, 2):
+            on_diagonal(step).start()
+            own(step).start()
+
+    @pl.when(jnp.logical_not(diagonal))
+    def _():
+        m_far.start()
+        m_near.start()
+        far(0).start()
+        near(0).start()
+        far(far_only).start()
+        near(near_only).start()
+        far(1).start()
+        near(1).start()
+
+    vm_remote.start()
+    v_remote.start()
+
+    vm_rows = vm.shape[1]
+    deep = depth // vm_rows
+
+    def mask_virt(base):
+        def one(b, _):
+            r = pl.ds(pl.multiple_of((base + b) * deep, deep), deep)
+            flags = vmask[pl.ds(base + b, 1), :]
+            vbuf[r, :] = vbuf[r, :] * jnp.broadcast_to(flags, (deep, cols)).astype(vbuf.dtype)
+            return 0
+
+        lax.fori_loop(0, vm_rows, one, 0)
+
+    width = cols // vm.shape[0]
+    vmask[pl.ds(pl.multiple_of(core * vm_rows, vm_rows), vm_rows), :] = spread(vm[...], width, True)
+    cmask[...] = spread(cm[...], cols // cm.shape[1])
+    vm_remote.wait_recv()
+    vmask[pl.ds(pl.multiple_of((1 - core) * vm_rows, vm_rows), vm_rows), :] = spread(vraw[...], width, True)
+    v_local.wait()
+    mask_virt(core * vm_rows)
+    for slot in range(2):
+        pltpu.make_async_copy(om, oraw.at[slot], m_recv.at[slot]).wait()
+        omask[slot] = spread(oraw[slot], occ.shape[1] // om.shape[1])
+    v_remote.wait_recv()
+    mask_virt((1 - core) * vm_rows)
+
+    tile = 256
+
+    def partial_copy(step):
+        return remote(pbuf.at[step], rbuf.at[step], p_send.at[step], p_recv.at[step], y_peer)
+
+    def z_copy(step):
+        dst = zbuf.at[tau, pl.ds((step % 2) * rows, rows), :]
+        return remote(cbuf.at[step], dst, z_send.at[step], z_recv.at[step], z_peer(step))
+
+    def flag_row(step):
+        return start_row(step) // block
+
+    def finish(step):
+        partial_copy(step).wait_recv()
+        flags = jnp.broadcast_to(cmask[pl.ds(flag_row(step), 1), :], (rows, cols))
+        chi = ((pa[step % 2] + rbuf[step].astype(jnp.float32)) * flags).astype(jnp.bfloat16)
+        if step < steps - 2:
+            cbuf[step] = chi
+            z_copy(step).start()
+        else:
+            zbuf[tau, pl.ds((step % 2) * rows, rows), :] = chi
+
+    for step in range(steps):
+        for slot in range(2):
+            if not (slot == 0 and step in (near_only, far_only)):
+                arrived(step, slot).wait()
+            elif step == near_only:
+                @pl.when(jnp.logical_not(diagonal))
+                def _():
+                    arrived(near_only, 0).wait()
+            else:
+                @pl.when(diagonal)
+                def _():
+                    arrived(far_only, 0).wait()
+            flags = omask[slot, pl.ds(flag_row(step), 1), :]
+            lhs[pl.ds(slot * rows, rows), :] = ob[step, slot] * jnp.broadcast_to(
+                flags, (rows, lhs.shape[1])
+            ).astype(lhs.dtype)
+
+        def one(n, _, step=step):
+            c = pl.ds(pl.multiple_of(n * tile, tile), tile)
+            r = jnp.dot(lhs[...], vbuf[:, c], preferred_element_type=jnp.float32)
+            pbuf[step, :, c] = r[:rows].astype(jnp.bfloat16)
+            pa[step % 2, :, c] = r[rows:]
+            return 0
+
+        lax.fori_loop(0, cols // tile, one, 0)
+        partial_copy(step).start()
+
+        @pl.when(diagonal)
+        def _(step=step):
+            if step == 0:
+                arrived(near_only, 0).wait()
+                forward(near_only).start()
+            for later in ((3, 4) if step == 0 else (step + 4,)):
+                if later < steps:
+                    on_diagonal(later).start()
+                    own(later).start()
+
+        @pl.when(jnp.logical_not(diagonal))
+        def _(step=step):
+            if step == 0:
+                arrived(far_only, 0).wait()
+                forward(far_only).start()
+            if step + 4 < steps:
+                far(step + 4).start()
+                near(step + 4).start()
+
+        if step > 0:
+            finish(step - 1)
+    finish(steps - 1)
+
+    for step in range(steps - 2):
+        z_copy(step).wait_recv()
+    for step in range(steps - 2):
+        z_copy(step).wait_send()
+    for step in range(steps):
+        partial_copy(step).wait_send()
+
+    @pl.when(diagonal)
+    def _():
+        for step in range(steps):
+            on_diagonal(step).wait_send()
+        forward(near_only).wait_send()
+        m_x.wait_send()
+
+    @pl.when(jnp.logical_not(diagonal))
+    def _():
+        for step in range(steps):
+            if step != near_only:
+                far(step).wait_send()
+            if step != far_only:
+                near(step).wait_send()
+        forward(far_only).wait_send()
+        m_far.wait_send()
+        m_near.wait_send()
+
+    v_remote.wait_send()
+    vm_remote.wait_send()
+
+
+def transform(w, z, out):
+    points = [z[t].astype(jnp.float32) for t in range(z.shape[0])]
+    for k in range(out.shape[0]):
+        total = w[k, 0] * points[0]
+        for t in range(1, len(points)):
+            total = total + w[k, t] * points[t]
+        out[k] = total
+
+
+def exchanged(taus, occupied, virtual_green, occ_mask, virt_mask, chi_mask, cosine_weights):
+    occ, virt = occupied[0], virtual_green[0]
+    m, k = occ.shape
+    depth, cols = virt.shape
+    rows = m // (2 * taus)
+    steps = 2 * taus
+    bf16, f32, i32 = jnp.bfloat16, jnp.float32, jnp.int32
+    dma = pltpu.SemaphoreType.DMA
+    vmem = pl.BlockSpec(memory_space=pltpu.VMEM)
+    vm = virt_mask.T
+    points = pl.pallas_call(
+        functools.partial(kernel, taus),
+        out_shape=jax.ShapeDtypeStruct((taus, 2 * rows, cols), bf16),
+        in_specs=[pl.BlockSpec(memory_space=pl.ANY), pl.BlockSpec(memory_space=pl.ANY), vmem, vmem, vmem],
+        out_specs=vmem,
+        scratch_shapes=[
+            pltpu.VMEM((2 * depth, cols), bf16),
+            pltpu.VMEM(vm.shape, i32),
+            pltpu.VMEM((2 * vm.shape[1], cols), f32),
+            pltpu.VMEM((steps, 2, rows, k), bf16),
+            pltpu.VMEM((2,) + occ_mask.shape, i32),
+            pltpu.VMEM((2, occ_mask.shape[0], k), f32),
+            pltpu.VMEM((chi_mask.shape[0], cols), f32),
+            pltpu.VMEM((2 * rows, k), bf16),
+            pltpu.VMEM((2, rows, cols), f32),
+            pltpu.VMEM((steps, rows, cols), bf16),
+            pltpu.VMEM((steps, rows, cols), bf16),
+            pltpu.VMEM((steps, rows, cols), bf16),
+            dma((5,)),
+            dma((steps, 2)),
+            dma((steps, 2)),
+            dma((1,)),
+            dma((2,)),
+            dma((2,)),
+            dma((steps,)),
+            dma((steps,)),
+            dma((steps,)),
+            dma((steps,)),
+        ],
+        compiler_params=pltpu.CompilerParams(collective_id=0, has_side_effects=True),
+    )(occ, virt, occ_mask, vm, chi_mask)
+    freqs = cosine_weights.shape[0]
+    return pl.pallas_call(
+        transform,
+        grid=(2,),
+        out_shape=jax.ShapeDtypeStruct((freqs, 2 * rows, cols), f32),
+        in_specs=[
+            pl.BlockSpec(memory_space=pltpu.SMEM),
+            pl.BlockSpec((taus, rows, cols), lambda i: (0, i, 0)),
+        ],
+        out_specs=pl.BlockSpec((freqs, rows, cols), lambda i: (0, i, 0)),
+    )(cosine_weights, points)
 
 
 def solution(mesh):
@@ -40,8 +339,9 @@
         P("row", "col"),
         P(),
     )
+    plane = mesh.shape["row"] == 4 and mesh.shape["col"] == 2 and mesh.shape["tau"] > 1
     return jax.shard_map(
-        shards,
+        functools.partial(exchanged, mesh.shape["tau"]) if plane else gathered,
         mesh=mesh,
         in_specs=placed,
         out_specs=P(None, ("row", "tau"), "col"),

time: 226 us -> 72.3 us (0.32)
  waiting for transfers between devices: 162 us -> 0 us
  Pallas kernels: 0 us -> 72.1 us
  blocking collectives: 19.3 us -> 0 us
  between operations: 13.5 us -> 0.01 us
  matrix products: 12.7 us -> 0 us
  other arithmetic: 11 us -> 0 us
  local copies, waits for them, and re-layouts: 7.38 us -> 0 us
    all_gather x2 -> x0, waiting for transfers between devices: 162 us -> none  [the longest x1 107 us: shards(): virt_column = lax.all_gather(virt_tile, 'row', axis=0, tiled=True)]
    pallas_call x0 -> x2, Pallas kernels: none -> 72.1 us  [the longest x1 70 us: exchanged(): pl.pallas_call(functools.partial(kernel, taus), out_shape=jax.ShapeDtypeS...]
    all_to_all x1 -> x0, blocking collectives: 19.3 us -> none  [shards(): lax.all_to_all(chi_local[None], 'tau', split_axis=1, concat_axis=0, tiled...]
    dot_general x2 -> x0, matrix products: 12.7 us -> none  [the longest x1 11.6 us: shards(): jnp.dot(lax.all_gather(occ_tile, 'col', axis=1, tiled=True), virt_column,...]
    mul x2 -> x0, other arithmetic: 6.35 us -> none  [expand_mask(): masked = shaped * flags.astype(values.dtype)[:, None, :, None]]
    unnamed x1 -> x0, other arithmetic: 3.95 us -> none
    unnamed x12 -> x0, local copies, waits for them, and re-layouts: 3.82 us -> none
  transfers between devices with their start and end apart: 2 -> 0, of which waited for: 2 -> 0; matrix products, arithmetic and copies ran while one was open for 1% -> 0% of each run, Pallas kernels for 0% -> 0%
where the time goes in v2:
time: 72.3 us; the launch traced here: 72.1 us
  Pallas kernels  72.1 us (100%)
    pallas_call x1, Pallas kernels, exchanged(): pl.pallas_call(functools.partial(kernel, taus), out_shape=jax.ShapeDtypeS...  70 us
    pallas_call x1, Pallas kernels, exchanged(): pl.pallas_call(transform, grid=(2,), out_shape=jax.ShapeDtypeStruct((freq...  2.09 us

profile of v2, /device:TPU:0, one launch (start us, length us, event | category | flops | bytes accessed | tf_op | source)
XLA Modules:
  0.0 72.1 jit_solution(2879445045459549513)
XLA Ops:
  0.0 70.0 %shard_map.64.z = bf16[4,64,1024]{2,1,0:T(8,128)(2,1)} custom-call(bf16[256,4096]{1,0:T(8,128)(2,1)} %bitcast.4, bf16[2048,1024]{1,0:T(8,128)(2,1)} %bitcast.3, s32[2,32]{1,0:T(2,128)} %om.1, s32[8,16]{1,0:T(8,128)} %bitcast.5, s32[2,8]{1,0:T(2,128)} %cm.1), custom_call_target="tpu_custom_call" | custom-call | tf_op jit(solution)/shard_map/pallas_call | solution.py:289
  70.1 2.1 %shard_map.65 = f32[4,64,1024]{2,1,0:T(8,128)} custom-call(f32[4,4]{1,0:T(4,128)} %w.1, bf16[4,64,1024]{2,1,0:T(8,128)(2,1)} %shard_map.64.z), custom_call_target="tpu_custom_call" | custom-call | tf_op jit(solution)/shard_map/pallas_call | solution.py:321

commit v3 on v2

--- a/solution.py
+++ b/solution.py
@@ -188,55 +188,64 @@
         else:
             zbuf[tau, pl.ds((step % 2) * rows, rows), :] = chi
 
-    for step in range(steps):
-        for slot in range(2):
-            if not (slot == 0 and step in (near_only, far_only)):
-                arrived(step, slot).wait()
-            elif step == near_only:
-                @pl.when(jnp.logical_not(diagonal))
-                def _():
-                    arrived(near_only, 0).wait()
-            else:
-                @pl.when(diagonal)
-                def _():
-                    arrived(far_only, 0).wait()
-            flags = omask[slot, pl.ds(flag_row(step), 1), :]
-            lhs[pl.ds(slot * rows, rows), :] = ob[step, slot] * jnp.broadcast_to(
-                flags, (rows, lhs.shape[1])
-            ).astype(lhs.dtype)
-
-        def one(n, _, step=step):
+    def load(step, slot):
+        def wait():
+            arrived(step, slot).wait()
+
+        if slot == 0 and step == near_only:
+            pl.when(jnp.logical_not(diagonal))(wait)
+        elif slot == 0 and step == far_only:
+            pl.when(diagonal)(wait)
+        else:
+            wait()
+        flags = omask[slot, pl.ds(flag_row(step), 1), :]
+        lhs[pl.ds(slot * rows, rows), :] = ob[step, slot] * jnp.broadcast_to(
+            flags, (rows, lhs.shape[1])
+        ).astype(lhs.dtype)
+
+    for step in range(-1, steps):
+        ahead = step + 1
+        first, last = step < 0, ahead == steps
+        if not last:
+            load(ahead, 0)
+        if not first:
+            load(step, 1)
+
+        def one(n, _, step=step, ahead=ahead, first=first, last=last):
             c = pl.ds(pl.multiple_of(n * tile, tile), tile)
-            r = jnp.dot(lhs[...], vbuf[:, c], preferred_element_type=jnp.float32)
-            pbuf[step, :, c] = r[:rows].astype(jnp.bfloat16)
-            pa[step % 2, :, c] = r[rows:]
+            base, end = (rows if last else 0), (rows if first else 2 * rows)
+            r = jnp.dot(lhs[base:end, :], vbuf[:, c], preferred_element_type=jnp.float32)
+            if not last:
+                pbuf[ahead, :, c] = r[:rows].astype(jnp.bfloat16)
+            if not first:
+                pa[step % 2, :, c] = r[rows - base :]
             return 0
 
         lax.fori_loop(0, cols // tile, one, 0)
-        partial_copy(step).start()
+        if not last:
+            partial_copy(ahead).start()
 
         @pl.when(diagonal)
-        def _(step=step):
-            if step == 0:
+        def _(ahead=ahead, first=first):
+            if first:
                 arrived(near_only, 0).wait()
                 forward(near_only).start()
-            for later in ((3, 4) if step == 0 else (step + 4,)):
+            for later in ((3, 4) if first else (ahead + 4,)):
                 if later < steps:
                     on_diagonal(later).start()
                     own(later).start()
 
         @pl.when(jnp.logical_not(diagonal))
-        def _(step=step):
-            if step == 0:
+        def _(ahead=ahead, first=first):
+            if first:
                 arrived(far_only, 0).wait()
                 forward(far_only).start()
-            if step + 4 < steps:
-                far(step + 4).start()
-                near(step + 4).start()
-
-        if step > 0:
-            finish(step - 1)
-    finish(steps - 1)
+            if ahead + 4 < steps:
+                far(ahead + 4).start()
+                near(ahead + 4).start()
+
+        if not first:
+            finish(step)
 
     for step in range(steps - 2):
         z_copy(step).wait_recv()

time: 72.3 us -> 72.4 us (level)
  no operation moved by 1% of the time
where the time goes in v3:
time: 72.4 us; the launch traced here: 72.2 us
  Pallas kernels  72.2 us (100%)
    pallas_call x1, Pallas kernels, exchanged(): pl.pallas_call(functools.partial(kernel, taus), out_shape=jax.ShapeDtypeS...  70.1 us
    pallas_call x1, Pallas kernels, exchanged(): pl.pallas_call(transform, grid=(2,), out_shape=jax.ShapeDtypeStruct((freq...  2.09 us

profile of v3, /device:TPU:0, one launch (start us, length us, event | category | flops | bytes accessed | tf_op | source)
XLA Modules:
  0.0 72.2 jit_solution(16077823583062286720)
XLA Ops:
  0.0 70.1 %shard_map.64.z = bf16[4,64,1024]{2,1,0:T(8,128)(2,1)} custom-call(bf16[256,4096]{1,0:T(8,128)(2,1)} %bitcast.4, bf16[2048,1024]{1,0:T(8,128)(2,1)} %bitcast.3, s32[2,32]{1,0:T(2,128)} %om.1, s32[8,16]{1,0:T(8,128)} %bitcast.5, s32[2,8]{1,0:T(2,128)} %cm.1), custom_call_target="tpu_custom_call" | custom-call | tf_op jit(solution)/shard_map/pallas_call | solution.py:298
  70.1 2.1 %shard_map.65 = f32[4,64,1024]{2,1,0:T(8,128)} custom-call(f32[4,4]{1,0:T(4,128)} %w.1, bf16[4,64,1024]{2,1,0:T(8,128)(2,1)} %shard_map.64.z), custom_call_target="tpu_custom_call" | custom-call | tf_op jit(solution)/shard_map/pallas_call | solution.py:330

commit v4 on v3

--- a/solution.py
+++ b/solution.py
@@ -53,7 +53,7 @@
 def kernel(
     taus, occ, virt, om, vm, cm, zbuf,
     vbuf, vraw, vmask, ob, oraw, omask, cmask, lhs, pa, pbuf, rbuf, cbuf,
-    v_sem, o_send, o_recv, f_send, m_send, m_recv, p_send, p_recv, z_send, z_recv,
+    v_sem, o_send, o_recv, h_recv, f_send, m_send, m_recv, p_send, p_recv, z_send, z_recv,
 ):
     tau, row, col = lax.axis_index("tau"), lax.axis_index("row"), lax.axis_index("col")
     half, core = row // 2, row % 2
@@ -69,6 +69,8 @@
     block = occ.shape[0] // om.shape[0]
     cols = virt.shape[1]
     near_only, far_only = 2, 3
+    shared = steps - 2
+    top, bottom = pl.ds(0, rows // 2), pl.ds(rows // 2, rows // 2)
 
     def start_row(step):
         return lax.rem(tau + 1 + step // 2, taus) * (2 * rows) + (step % 2) * rows
@@ -108,6 +110,23 @@
 
     def forward(step):
         return remote(ob.at[step, 0], ob.at[step, 0], f_send.at[0], o_recv.at[step, 0], x_peer)
+
+    def half_src(side):
+        at = start_row(shared) + side * (rows // 2)
+        return occ.at[pl.ds(pl.multiple_of(at, rows // 2), rows // 2), :]
+
+    def half_near():
+        return remote(half_src(0), ob.at[shared, 0, top], o_send.at[shared, 0], h_recv.at[0], y_peer)
+
+    def half_far():
+        return remote(half_src(1), ob.at[shared, 0, bottom], o_send.at[shared, 1], h_recv.at[1], far_peer)
+
+    def half_forward(side):
+        part = ob.at[shared, 0, bottom if side else top]
+        return remote(part, part, f_send.at[1], h_recv.at[side], x_peer)
+
+    def half_arrived(side):
+        return pltpu.make_async_copy(half_src(side), ob.at[shared, 0, bottom if side else top], h_recv.at[side])
 
     def arrived(step, slot):
         return pltpu.make_async_copy(o_src(step), ob.at[step, slot], o_recv.at[step, slot])
@@ -123,7 +142,7 @@
     def _():
         m_x.start()
         m_own.start()
-        for step in (0, 1, 2):
+        for step in range(4):
             on_diagonal(step).start()
             own(step).start()
 
@@ -137,6 +156,11 @@
         near(near_only).start()
         far(1).start()
         near(1).start()
+        half_far().start()
+        half_near().start()
+        for step in range(4, 6):
+            far(step).start()
+            near(step).start()
 
     vm_remote.start()
     v_remote.start()
@@ -168,8 +192,11 @@
 
     tile = 256
 
-    def partial_copy(step):
-        return remote(pbuf.at[step], rbuf.at[step], p_send.at[step], p_recv.at[step], y_peer)
+    def partial_copy(step, side):
+        part = pl.ds(side * (cols // 2), cols // 2)
+        return remote(
+            pbuf.at[step, :, part], rbuf.at[step, :, part], p_send.at[step, side], p_recv.at[step, side], y_peer
+        )
 
     def z_copy(step):
         dst = zbuf.at[tau, pl.ds((step % 2) * rows, rows), :]
@@ -179,7 +206,8 @@
         return start_row(step) // block
 
     def finish(step):
-        partial_copy(step).wait_recv()
+        partial_copy(step, 0).wait_recv()
+        partial_copy(step, 1).wait_recv()
         flags = jnp.broadcast_to(cmask[pl.ds(flag_row(step), 1), :], (rows, cols))
         chi = ((pa[step % 2] + rbuf[step].astype(jnp.float32)) * flags).astype(jnp.bfloat16)
         if step < steps - 2:
@@ -196,6 +224,9 @@
             pl.when(jnp.logical_not(diagonal))(wait)
         elif slot == 0 and step == far_only:
             pl.when(diagonal)(wait)
+        elif slot == 0 and step == shared:
+            pl.when(diagonal)(lambda: half_arrived(1).wait())
+            pl.when(jnp.logical_not(diagonal))(lambda: half_arrived(0).wait())
         else:
             wait()
         flags = omask[slot, pl.ds(flag_row(step), 1), :]
@@ -221,16 +252,23 @@
                 pa[step % 2, :, c] = r[rows - base :]
             return 0
 
-        lax.fori_loop(0, cols // tile, one, 0)
+        halves = cols // tile // 2
+        lax.fori_loop(0, halves, one, 0)
         if not last:
-            partial_copy(ahead).start()
+            partial_copy(ahead, 0).start()
+        lax.fori_loop(halves, 2 * halves, one, 0)
+        if not last:
+            partial_copy(ahead, 1).start()
 
         @pl.when(diagonal)
         def _(ahead=ahead, first=first):
             if first:
                 arrived(near_only, 0).wait()
                 forward(near_only).start()
-            for later in ((3, 4) if first else (ahead + 4,)):
+            if ahead == 2:
+                half_arrived(0).wait()
+                half_forward(0).start()
+            for later in (range(4, 6) if first else range(6, steps) if ahead == 2 else ()):
                 if later < steps:
                     on_diagonal(later).start()
                     own(later).start()
@@ -240,9 +278,12 @@
             if first:
                 arrived(far_only, 0).wait()
                 forward(far_only).start()
-            if ahead + 4 < steps:
-                far(ahead + 4).start()
-                near(ahead + 4).start()
+            if ahead == 2:
+                half_arrived(1).wait()
+                half_forward(1).start()
+            if ahead + 6 < steps and ahead + 6 != shared:
+                far(ahead + 6).start()
+                near(ahead + 6).start()
 
         if not first:
             finish(step)
@@ -252,23 +293,28 @@
     for step in range(steps - 2):
         z_copy(step).wait_send()
     for step in range(steps):
-        partial_copy(step).wait_send()
+        partial_copy(step, 0).wait_send()
+        partial_copy(step, 1).wait_send()
 
     @pl.when(diagonal)
     def _():
         for step in range(steps):
             on_diagonal(step).wait_send()
         forward(near_only).wait_send()
+        half_forward(0).wait_send()
         m_x.wait_send()
 
     @pl.when(jnp.logical_not(diagonal))
     def _():
         for step in range(steps):
-            if step != near_only:
+            if step not in (near_only, shared):
                 far(step).wait_send()
-            if step != far_only:
+            if step not in (far_only, shared):
                 near(step).wait_send()
+        half_far().wait_send()
+        half_near().wait_send()
         forward(far_only).wait_send()
+        half_forward(1).wait_send()
         m_far.wait_send()
         m_near.wait_send()
 
@@ -316,11 +362,12 @@
             dma((5,)),
             dma((steps, 2)),
             dma((steps, 2)),
-            dma((1,)),
             dma((2,)),
             dma((2,)),
-            dma((steps,)),
-            dma((steps,)),
+            dma((2,)),
+            dma((2,)),
+            dma((steps, 2)),
+            dma((steps, 2)),
             dma((steps,)),
             dma((steps,)),
         ],
@@ -348,7 +395,7 @@
         P("row", "col"),
         P(),
     )
-    plane = mesh.shape["row"] == 4 and mesh.shape["col"] == 2 and mesh.shape["tau"] > 1
+    plane = mesh.shape["row"] == 4 and mesh.shape["col"] == 2 and mesh.shape["tau"] > 3
     return jax.shard_map(
         functools.partial(exchanged, mesh.shape["tau"]) if plane else gathered,
         mesh=mesh,

time: 72.4 us -> 66.3 us (0.916)
  Pallas kernels: 72.2 us -> 66.1 us
    pallas_call x1, Pallas kernels: 70.1 us -> 64 us  [exchanged(): pl.pallas_call(functools.partial(kernel, taus), out_shape=jax.ShapeDtypeS...]
where the time goes in v4:
time: 66.3 us; the launch traced here: 66.1 us
  Pallas kernels  66.1 us (100%)
    pallas_call x1, Pallas kernels, exchanged(): pl.pallas_call(functools.partial(kernel, taus), out_shape=jax.ShapeDtypeS...  64 us
    pallas_call x1, Pallas kernels, exchanged(): pl.pallas_call(transform, grid=(2,), out_shape=jax.ShapeDtypeStruct((freq...  2.09 us

profile of v4, /device:TPU:0, one launch (start us, length us, event | category | flops | bytes accessed | tf_op | source)
XLA Modules:
  0.0 66.1 jit_solution(5618212767384350617)
XLA Ops:
  0.0 64.0 %shard_map.64.z = bf16[4,64,1024]{2,1,0:T(8,128)(2,1)} custom-call(bf16[256,4096]{1,0:T(8,128)(2,1)} %bitcast.4, bf16[2048,1024]{1,0:T(8,128)(2,1)} %bitcast.3, s32[2,32]{1,0:T(2,128)} %om.1, s32[8,16]{1,0:T(8,128)} %bitcast.5, s32[2,8]{1,0:T(2,128)} %cm.1), custom_call_target="tpu_custom_call" | custom-call | tf_op jit(solution)/shard_map/pallas_call | solution.py:344
  64.0 2.1 %shard_map.65 = f32[4,64,1024]{2,1,0:T(8,128)} custom-call(f32[4,4]{1,0:T(4,128)} %w.1, bf16[4,64,1024]{2,1,0:T(8,128)(2,1)} %shard_map.64.z), custom_call_target="tpu_custom_call" | custom-call | tf_op jit(solution)/shard_map/pallas_call | solution.py:377

commit v5 on v4

--- a/solution.py
+++ b/solution.py
@@ -68,7 +68,7 @@
     depth = virt.shape[0]
     block = occ.shape[0] // om.shape[0]
     cols = virt.shape[1]
-    near_only, far_only = 2, 3
+    near_only, far_only = 3, 2
     shared = steps - 2
     top, bottom = pl.ds(0, rows // 2), pl.ds(rows // 2, rows // 2)
 
@@ -158,7 +158,7 @@
         near(1).start()
         half_far().start()
         half_near().start()
-        for step in range(4, 6):
+        for step in range(4, 5):
             far(step).start()
             near(step).start()
 
@@ -281,9 +281,9 @@
             if ahead == 2:
                 half_arrived(1).wait()
                 half_forward(1).start()
-            if ahead + 6 < steps and ahead + 6 != shared:
-                far(ahead + 6).start()
-                near(ahead + 6).start()
+            if ahead + 5 < steps and ahead + 5 != shared:
+                far(ahead + 5).start()
+                near(ahead + 5).start()
 
         if not first:
             finish(step)
@@ -343,7 +343,7 @@
     vm = virt_mask.T
     points = pl.pallas_call(
         functools.partial(kernel, taus),
-        out_shape=jax.ShapeDtypeStruct((taus, 2 * rows, cols), bf16),
+        out_shape=pltpu.VMEM((taus, 2 * rows, cols), bf16),
         in_specs=[pl.BlockSpec(memory_space=pl.ANY), pl.BlockSpec(memory_space=pl.ANY), vmem, vmem, vmem],
         out_specs=vmem,
         scratch_shapes=[

time: 66.3 us -> 66.3 us (level)
  Pallas kernels: 66.1 us -> 65.3 us
  local copies, waits for them, and re-layouts: 0 us -> 0.78 us
    pallas_call x1, Pallas kernels: 64 us -> 63.2 us  [exchanged(): pl.pallas_call(functools.partial(kernel, taus), out_shape=pltpu.VMEM((tau...]
    unnamed x0 -> x2, local copies, waits for them, and re-layouts: none -> 0.78 us
where the time goes in v5:
time: 66.3 us; the launch traced here: 66.1 us
  Pallas kernels  65.3 us (98%)
  local copies, waits for them, and re-layouts  0.78 us (1%)
    pallas_call x1, Pallas kernels, exchanged(): pl.pallas_call(functools.partial(kernel, taus), out_shape=pltpu.VMEM((tau...  63.2 us
    pallas_call x1, Pallas kernels, exchanged(): pl.pallas_call(transform, grid=(2,), out_shape=jax.ShapeDtypeStruct((freq...  2.07 us

profile of v5, /device:TPU:0, one launch (start us, length us, event | category | flops | bytes accessed | tf_op | source)
XLA Modules:
  0.0 66.1 jit_solution(3829156788161702813)
XLA Ops:
  0.0 63.2 %shard_map.64.z = bf16[4,64,1024]{2,1,0:T(8,128)(2,1)S(1)} custom-call(bf16[256,4096]{1,0:T(8,128)(2,1)} %bitcast.4, bf16[2048,1024]{1,0:T(8,128)(2,1)} %bitcast.3, s32[2,32]{1,0:T(2,128)} %om.1, s32[8,16]{1,0:T(8,128)} %bitcast.5, s32[2,8]{1,0:T(2,128)} %cm.1), custom_call_target="tpu_custom_call" | custom-call | tf_op jit(solution)/shard_map/pallas_call | solution.py:344
  63.2 0.0 copy-start
  63.2 0.8 %copy-done = bf16[4,64,1024]{2,1,0:T(8,128)(2,1)} copy-done((bf16[4,64,1024]{2,1,0:T(8,128)(2,1)}, bf16[4,64,1024]{2,1,0:T(8,128)(2,1)S(1)}, u32[]{:S(2)}) %copy-start) | copy-done | bytes 524312
  64.0 2.1 %shard_map.65 = f32[4,64,1024]{2,1,0:T(8,128)} custom-call(f32[4,4]{1,0:T(4,128)} %w.1, bf16[4,64,1024]{2,1,0:T(8,128)(2,1)} %copy-done), custom_call_target="tpu_custom_call" | custom-call | tf_op jit(solution)/shard_map/pallas_call | solution.py:377
Async XLA Ops:
  63.2 0.8 %copy-start = (bf16[4,64,1024]{2,1,0:T(8,128)(2,1)}, bf16[4,64,1024]{2,1,0:T(8,128)(2,1)S(1)}, u32[]{:S(2)}) copy-start(bf16[4,64,1024]{2,1,0:T(8,128)(2,1)S(1)} %shard_map.64.z) | copy-start | bytes 1572868
